TPU v7x, 32 devices: a whole 2x2x4 slice. The times are simulated.
32 devices in a mesh: shift: 2 (over y), expert: 4 (over z), shard: 4 (over x, core).
Axes of the slice: x: 2, y: 2, z: 4, core: 2. Of those that a mesh axis runs over, the one named last changes fastest.
Arguments:
- master_gate: float32 [128, 2048, 1024], P(('shift', 'expert'), 'shard'), parts along dimension 0, may hold values from -0.1875 to 0.1875
- master_up: float32 [128, 2048, 1024], P(('shift', 'expert'), 'shard'), parts along dimension 0, may hold values from -0.1875 to 0.1875
- router_weight: float32 [4096, 64], P(('shift', 'shard'), 'expert'), parts along dimension 0, may hold values from -0.125 to 0.125
- router_gain: float32 [4096], P(('shift', 'shard')), parts along dimension 0, may hold values from 0.25 to 1.75
Outputs:
- final_gate: bfloat16 [128, 2048, 1024], P(('shift', 'expert'), None, 'shard'), parts along dimension 0
- final_up: bfloat16 [128, 2048, 1024], P(('shift', 'expert'), None, 'shard'), parts along dimension 0
- scale_gate: float32 [128, 1024], P(('shift', 'expert'), 'shard'), parts along dimension 0
- scale_up: float32 [128, 1024], P(('shift', 'expert'), 'shard'), parts along dimension 0
- serve_router: bfloat16 [4096, 64], P('shift'), parts along dimension 0
There are 2 independent parts, one for each index of `shift`. A program takes and returns all parts, laid end to end along the dimension named above; each array names one. Nothing has to cross between parts.
All inputs are finite; a program needn't handle non-finite values. Where the computation divides by a largest or mean magnitude, that divisor is 1e-20 or more.
Results may differ from a plain program's by a relative error of at most 0.001.
Values may be sent and summed in bfloat16 or wider, within the bound.
No kernel may reach another device: no remote copies, remote signals or barrier semaphores. Data moves between devices by JAX's collectives and lax.ppermute only.
A program may use at most 256 MiB of HBM per device.

v0:
```python
import jax
import jax.numpy as jnp
from jax import lax
from jax.sharding import PartitionSpec as P


def shards(master_gate, master_up, router_weight, router_gain):
    scale_gate, scale_up = lax.pmax(
        (jnp.max(jnp.abs(master_gate), axis=1), jnp.max(jnp.abs(master_up), axis=1)), "shard"
    )
    narrow_gate, narrow_up = (
        (master_gate / jnp.expand_dims(scale_gate, 1)).astype(jnp.bfloat16),
        (master_up / jnp.expand_dims(scale_up, 1)).astype(jnp.bfloat16),
    )
    final_gate, final_up = (
        lax.all_to_all(narrow_gate, "shard", split_axis=2, concat_axis=1, tiled=True),
        lax.all_to_all(narrow_up, "shard", split_axis=2, concat_axis=1, tiled=True),
    )
    scale_gate = lax.dynamic_slice_in_dim(
        scale_gate, lax.axis_index("shard") * final_gate.shape[2], final_gate.shape[2], axis=1
    )
    scale_up = lax.dynamic_slice_in_dim(
        scale_up, lax.axis_index("shard") * final_up.shape[2], final_up.shape[2], axis=1
    )
    part_router = (router_weight * router_gain[:, None]).astype(jnp.bfloat16)
    row_router = lax.all_gather(part_router, "shard", axis=0, tiled=True)
    serve_router = lax.all_gather(row_router, "expert", axis=1, tiled=True)
    return (final_gate, final_up, scale_gate, scale_up, serve_router)


def solution(mesh):
    in_specs = (
        P(("shift", "expert"), "shard", None),
        P(("shift", "expert"), "shard", None),
        P(("shift", "shard"), "expert"),
        P(("shift", "shard")),
    )
    out_specs = (
        P(("shift", "expert"), None, "shard"),
        P(("shift", "expert"), None, "shard"),
        P(("shift", "expert"), "shard"),
        P(("shift", "expert"), "shard"),
        P("shift", None),
    )
    return jax.shard_map(shards, mesh=mesh, in_specs=in_specs, out_specs=out_specs, check_vma=False)
```

profile of v0, /device:TPU:0, one launch (start us, length us, event | category | flops | bytes accessed | tf_op | source)
XLA Modules:
  0.0 541.3 jit_solution(9778503414393642907)
XLA Ops:
  7.2 0.0 all-reduce.3.cloned.1.call-start
  7.2 0.0 copy-start
  7.2 12.6 %abs_reduce_fusion = f32[16,1024]{1,0:T(8,128)} fusion(f32[16,512,1024]{2,1,0:T(8,128)} %param.5), kind=kLoop, calls=%fused_computation.1 | loop fusion | flops 16760832 | bytes 33619968 | tf_op jit(solution)/shard_map/reduce_max | solution.py:9
  19.8 7.6 %copy-done = f32[16,512,1024]{2,1,0:T(8,128)S(1)} copy-done((f32[16,512,1024]{2,1,0:T(8,128)S(1)}, f32[16,512,1024]{2,1,0:T(8,128)}, u32[]{:S(2)}) %copy-start) | copy-done | bytes 33554456
  27.4 2.7 abs_reduce_fusion.1
  30.1 0.0 all-reduce.3.cloned.1.call-update
  30.2 34.2 %copy.12 = f32[16,512,1024]{1,0,2:T(8,128)} copy(f32[16,512,1024]{2,1,0:T(8,128)} %param.4) | data formatting | bytes 67108864 | tf_op args[0]
  64.4 0.5 all-reduce.3.cloned.1.call-done
  64.9 1.0 copy.11
  66.0 17.7 %divide_convert_fusion.1 = bf16[16,512,1024]{1,0,2:T(8,128)(2,1)} fusion(f32[16,512,1024]{1,0,2:T(8,128)} %copy.12, f32[16,1024]{0,1:T(8,128)S(1)} %copy.11), kind=kLoop, calls=%fused_computation.2 | loop fusion | flops 16777216 | bytes 50397184 | tf_op jit(solution)/shard_map/convert_element_type | solution.py:12
  83.6 7.1 %all-to-all-start = ((bf16[16,512,1024]{1,0,2:T(8,128)(2,1)}), bf16[16,512,1024]{1,0,2:T(8,128)(2,1)}, u32[]{:S(2)}, u32[]{:S(2)}) async-start(bf16[16,512,1024]{1,0,2:T(8,128)(2,1)} %divide_convert_fusion.1), calls=%async_computation | async-start | bytes 33554432 | tf_op jit(solution)/shard_map/all_to_all | solution.py:16
  90.7 0.0 copy-start.1
  90.7 34.2 %copy.15 = f32[16,512,1024]{1,0,2:T(8,128)} copy(f32[16,512,1024]{2,1,0:T(8,128)} %param.5) | data formatting | bytes 67108864 | tf_op args[1]
  124.9 0.0 copy-done.1
  124.9 0.2 copy.14
  125.1 0.0 copy-start.2
  125.1 0.0 copy-start.3
  125.2 17.7 %divide_convert_fusion = bf16[16,512,1024]{1,0,2:T(8,128)(2,1)} fusion(f32[16,512,1024]{1,0,2:T(8,128)} %copy.15, f32[16,1024]{0,1:T(8,128)S(1)} %copy.14), kind=kLoop, calls=%fused_computation | loop fusion | flops 16777216 | bytes 50397184 | tf_op jit(solution)/shard_map/convert_element_type | solution.py:13
  142.8 131.1 %all-to-all-done = bf16[16,512,1024]{1,0,2:T(8,128)(2,1)} async-done(((bf16[16,512,1024]{1,0,2:T(8,128)(2,1)}), bf16[16,512,1024]{1,0,2:T(8,128)(2,1)}, u32[]{:S(2)}, u32[]{:S(2)}) %all-to-all-start) | async-done | bytes 16777248 | tf_op jit(solution)/shard_map/all_to_all | solution.py:16
  273.9 7.0 %all-to-all-start.1 = ((bf16[16,512,1024]{1,0,2:T(8,128)(2,1)}), bf16[16,512,1024]{1,0,2:T(8,128)(2,1)}, u32[]{:S(2)}, u32[]{:S(2)}) async-start(bf16[16,512,1024]{1,0,2:T(8,128)(2,1)} %divide_convert_fusion), calls=%async_computation.1 | async-start | bytes 33554432 | tf_op jit(solution)/shard_map/all_to_all | solution.py:17
  280.9 0.0 copy-done.2
  280.9 0.0 copy-done.3
  280.9 184.1 %all_gather.6 = bf16[2048,16]{0,1:T(8,128)(2,1)S(1)} all-gather(bf16[512,16]{0,1:T(8,128)(2,1)S(1)} %multiply_convert_fusion), channel_id=1, replica_groups=mesh['shift'=2,'expert'=4,'shard'=4] {'shard'}, dimensions={0}, use_global_device_ids=true | all-gather | bytes 81920 | tf_op jit(solution)/shard_map/all_gather | solution.py:26
  465.0 15.1 %all_gather.7 = bf16[2048,64]{0,1:T(8,128)(2,1)S(1)} all-gather(bf16[2048,16]{0,1:T(8,128)(2,1)S(1)} %all_gather.6), channel_id=1, replica_groups=mesh['shift'=2,'expert'=4,'shard'=4] {'expert'}, dimensions={1}, use_global_device_ids=true | all-gather | bytes 327680 | tf_op jit(solution)/shard_map/all_gather | solution.py:27
  480.1 1.3 constant_dynamic-slice_fusion
  481.4 26.2 %copy.13 = bf16[16,4,512,256]{3,2,1,0:T(8,128)(2,1)} copy(bf16[16,4,512,256]{2,0,3,1:T(8,128)(2,1)} %bitcast.1) | data formatting | bytes 33554432 | tf_op jit(solution)/shard_map/all_to_all | solution.py:16
  507.6 0.0 all-to-all-done.1
  507.6 26.2 %copy.16 = bf16[16,4,512,256]{3,2,1,0:T(8,128)(2,1)} copy(bf16[16,4,512,256]{2,0,3,1:T(8,128)(2,1)} %bitcast.4) | data formatting | bytes 33554432 | tf_op jit(solution)/shard_map/all_to_all | solution.py:17
  533.8 0.7 copy.20
  (1 shorter events, 0.0 us)
Async XLA Ops:
  7.2 57.7 %all-reduce.3.cloned.1.call-start = ((), (), s32[]{:S(2)}) async-start(), calls=%async_computation.2 | async-start | bytes 262144 | tf_op jit(solution)/shard_map/pmax | solution.py:8
  7.2 20.2 %copy-start = (f32[16,512,1024]{2,1,0:T(8,128)S(1)}, f32[16,512,1024]{2,1,0:T(8,128)}, u32[]{:S(2)}) copy-start(f32[16,512,1024]{2,1,0:T(8,128)} %param.4) | copy-start | bytes 100663296
  83.6 190.3 %all-to-all-start = ((bf16[16,512,1024]{1,0,2:T(8,128)(2,1)}), bf16[16,512,1024]{1,0,2:T(8,128)(2,1)}, u32[]{:S(2)}, u32[]{:S(2)}) async-start(bf16[16,512,1024]{1,0,2:T(8,128)(2,1)} %divide_convert_fusion.1), calls=%async_computation | async-start | bytes 33554432 | tf_op jit(solution)/shard_map/all_to_all | solution.py:16
  90.7 34.2 %copy-start.1 = (f32[16,1024]{1,0:T(8,128)S(1)}, f32[16,1024]{1,0:T(8,128)}, u32[]{:S(2)}) copy-start(f32[16,1024]{1,0:T(8,128)} %get-tuple-element.6) | copy-start | bytes 196612
  125.1 155.7 %copy-start.2 = (f32[512,16]{0,1:T(8,128)S(1)}, f32[512,16]{0,1:T(8,128)}, u32[]{:S(2)}) copy-start(f32[512,16]{0,1:T(8,128)} %param.6) | copy-start | bytes 98308
  125.1 155.7 %copy-start.3 = (f32[512]{0:T(512)S(1)}, f32[512]{0:T(512)}, u32[]{:S(2)}) copy-start(f32[512]{0:T(512)} %param.7) | copy-start | bytes 6148
  273.9 233.7 %all-to-all-start.1 = ((bf16[16,512,1024]{1,0,2:T(8,128)(2,1)}), bf16[16,512,1024]{1,0,2:T(8,128)(2,1)}, u32[]{:S(2)}, u32[]{:S(2)}) async-start(bf16[16,512,1024]{1,0,2:T(8,128)(2,1)} %divide_convert_fusion), calls=%async_computation.1 | async-start | bytes 33554432 | tf_op jit(solution)/shard_map/all_to_all | solution.py:17
Sparse Core Ops, SparseCore 0:
  30.3 34.5 all-reduce.2
where the time goes:
time: 544 us; the launch traced here: 541 us
  blocking collectives  199 us (37%)
  local copies, waits for them, and re-layouts  132 us (24%)
  waiting for transfers between devices  132 us (24%)
  other arithmetic  50.7 us (9%)
  starting transfers between devices  14.1 us (3%)
  between operations  14.1 us (3%)
    all_gather x1, blocking collectives, shards(): row_router = lax.all_gather(part_router, 'shard', axis=0, tiled=True)  184 us
    all_to_all x1, waiting for transfers between devices, shards(): lax.all_to_all(narrow_gate, 'shard', split_axis=2, concat_axis=1, tiled=T...  131 us
    unnamed x11, local copies, waits for them, and re-layouts  76.7 us
    all_to_all x1, local copies, waits for them, and re-layouts, shards(): lax.all_to_all(narrow_up, 'shard', split_axis=2, concat_axis=1, tiled=True)  26.2 us
    all_to_all x1, local copies, waits for them, and re-layouts, shards(): lax.all_to_all(narrow_gate, 'shard', split_axis=2, concat_axis=1, tiled=T...  26.2 us
    convert_element_type x1, other arithmetic, shards(): (master_gate / jnp.expand_dims(scale_gate, 1)).astype(jnp.bfloat16)  17.7 us
    convert_element_type x1, other arithmetic, shards(): (master_up / jnp.expand_dims(scale_up, 1)).astype(jnp.bfloat16)  17.7 us
    all_gather x1, blocking collectives, shards(): serve_router = lax.all_gather(row_router, 'expert', axis=1, tiled=True)  15.1 us
  transfers between devices with their start and end apart: 3, of which 2 were waited for; matrix products, arithmetic and copies ran while one was open for 21% of the time, Pallas kernels for 0%

commit v1 on v0

--- a/solution.py
+++ b/solution.py
@@ -24,7 +24,8 @@
     )
     part_router = (router_weight * router_gain[:, None]).astype(jnp.bfloat16)
     row_router = lax.all_gather(part_router, "shard", axis=0, tiled=True)
-    serve_router = lax.all_gather(row_router, "expert", axis=1, tiled=True)
+    parts = lax.all_gather(row_router, "expert", axis=0, tiled=False)
+    serve_router = jnp.concatenate(parts, axis=1)
     return (final_gate, final_up, scale_gate, scale_up, serve_router)
 
 

time: 544 us -> 544 us (level)
    unnamed x11 -> x10, local copies, waits for them, and re-layouts: 76.7 us -> 76 us
where the time goes in v1:
time: 544 us; the launch traced here: 541 us
  blocking collectives  199 us (37%)
  local copies, waits for them, and re-layouts  132 us (24%)
  waiting for transfers between devices  132 us (24%)
  other arithmetic  50.7 us (9%)
  starting transfers between devices  14.1 us (3%)
  between operations  14.1 us (3%)
    all_gather x1, blocking collectives, shards(): row_router = lax.all_gather(part_router, 'shard', axis=0, tiled=True)  184 us
    all_to_all x1, waiting for transfers between devices, shards(): lax.all_to_all(narrow_gate, 'shard', split_axis=2, concat_axis=1, tiled=T...  131 us
    unnamed x10, local copies, waits for them, and re-layouts  76 us
    all_to_all x1, local copies, waits for them, and re-layouts, shards(): lax.all_to_all(narrow_up, 'shard', split_axis=2, concat_axis=1, tiled=True)  26.2 us
    all_to_all x1, local copies, waits for them, and re-layouts, shards(): lax.all_to_all(narrow_gate, 'shard', split_axis=2, concat_axis=1, tiled=T...  26.2 us
    convert_element_type x1, other arithmetic, shards(): (master_gate / jnp.expand_dims(scale_gate, 1)).astype(jnp.bfloat16)  17.7 us
    convert_element_type x1, other arithmetic, shards(): (master_up / jnp.expand_dims(scale_up, 1)).astype(jnp.bfloat16)  17.7 us
    all_gather x1, blocking collectives, shards(): parts = lax.all_gather(row_router, 'expert', axis=0, tiled=False)  15.1 us
  transfers between devices with their start and end apart: 3, of which 2 were waited for; matrix products, arithmetic and copies ran while one was open for 21% of the time, Pallas kernels for 0%

profile of v1, /device:TPU:0, one launch (start us, length us, event | category | flops | bytes accessed | tf_op | source)
XLA Modules:
  0.0 541.3 jit_solution(6056821258190931910)
XLA Ops:
  7.2 0.0 all-reduce.3.cloned.1.call-start
  7.2 0.0 copy-start
  7.2 12.6 %abs_reduce_fusion = f32[16,1024]{1,0:T(8,128)} fusion(f32[16,512,1024]{2,1,0:T(8,128)} %param.5), kind=kLoop, calls=%fused_computation.1 | loop fusion | flops 16760832 | bytes 33619968 | tf_op jit(solution)/shard_map/reduce_max | solution.py:9
  19.8 7.6 %copy-done = f32[16,512,1024]{2,1,0:T(8,128)S(1)} copy-done((f32[16,512,1024]{2,1,0:T(8,128)S(1)}, f32[16,512,1024]{2,1,0:T(8,128)}, u32[]{:S(2)}) %copy-start) | copy-done | bytes 33554456
  27.4 2.7 abs_reduce_fusion.1
  30.1 0.0 all-reduce.3.cloned.1.call-update
  30.2 34.2 %copy.13 = f32[16,512,1024]{1,0,2:T(8,128)} copy(f32[16,512,1024]{2,1,0:T(8,128)} %param.4) | data formatting | bytes 67108864 | tf_op args[0]
  64.4 0.5 all-reduce.3.cloned.1.call-done
  64.9 1.0 copy.12
  66.0 17.7 %divide_convert_fusion.1 = bf16[16,512,1024]{1,0,2:T(8,128)(2,1)} fusion(f32[16,512,1024]{1,0,2:T(8,128)} %copy.13, f32[16,1024]{0,1:T(8,128)S(1)} %copy.12), kind=kLoop, calls=%fused_computation.2 | loop fusion | flops 16777216 | bytes 50397184 | tf_op jit(solution)/shard_map/convert_element_type | solution.py:12
  83.6 7.1 %all-to-all-start = ((bf16[16,512,1024]{1,0,2:T(8,128)(2,1)}), bf16[16,512,1024]{1,0,2:T(8,128)(2,1)}, u32[]{:S(2)}, u32[]{:S(2)}) async-start(bf16[16,512,1024]{1,0,2:T(8,128)(2,1)} %divide_convert_fusion.1), calls=%async_computation | async-start | bytes 33554432 | tf_op jit(solution)/shard_map/all_to_all | solution.py:16
  90.7 0.0 copy-start.1
  90.7 34.2 %copy.16 = f32[16,512,1024]{1,0,2:T(8,128)} copy(f32[16,512,1024]{2,1,0:T(8,128)} %param.5) | data formatting | bytes 67108864 | tf_op args[1]
  124.9 0.0 copy-done.1
  124.9 0.2 copy.15
  125.1 0.0 copy-start.2
  125.1 0.0 copy-start.3
  125.2 17.7 %divide_convert_fusion = bf16[16,512,1024]{1,0,2:T(8,128)(2,1)} fusion(f32[16,512,1024]{1,0,2:T(8,128)} %copy.16, f32[16,1024]{0,1:T(8,128)S(1)} %copy.15), kind=kLoop, calls=%fused_computation | loop fusion | flops 16777216 | bytes 50397184 | tf_op jit(solution)/shard_map/convert_element_type | solution.py:13
  142.8 131.1 %all-to-all-done = bf16[16,512,1024]{1,0,2:T(8,128)(2,1)} async-done(((bf16[16,512,1024]{1,0,2:T(8,128)(2,1)}), bf16[16,512,1024]{1,0,2:T(8,128)(2,1)}, u32[]{:S(2)}, u32[]{:S(2)}) %all-to-all-start) | async-done | bytes 16777248 | tf_op jit(solution)/shard_map/all_to_all | solution.py:16
  273.9 7.0 %all-to-all-start.1 = ((bf16[16,512,1024]{1,0,2:T(8,128)(2,1)}), bf16[16,512,1024]{1,0,2:T(8,128)(2,1)}, u32[]{:S(2)}, u32[]{:S(2)}) async-start(bf16[16,512,1024]{1,0,2:T(8,128)(2,1)} %divide_convert_fusion), calls=%async_computation.1 | async-start | bytes 33554432 | tf_op jit(solution)/shard_map/all_to_all | solution.py:17
  280.9 0.0 copy-done.2
  280.9 0.0 copy-done.3
  280.9 184.1 %all_gather.9 = bf16[2048,16]{0,1:T(8,128)(2,1)S(1)} all-gather(bf16[512,16]{0,1:T(8,128)(2,1)S(1)} %multiply_convert_fusion), channel_id=1, replica_groups=mesh['shift'=2,'expert'=4,'shard'=4] {'shard'}, dimensions={0}, use_global_device_ids=true | all-gather | bytes 81920 | tf_op jit(solution)/shard_map/all_gather | solution.py:26
  465.0 15.1 %all-gather = bf16[8192,16]{0,1:T(8,128)(2,1)S(1)} all-gather(bf16[2048,16]{0,1:T(8,128)(2,1)S(1)} %all_gather.9), channel_id=2, replica_groups=mesh['shift'=2,'expert'=4,'shard'=4] {'expert'}, dimensions={0}, use_global_device_ids=true | all-gather | bytes 327680 | tf_op jit(solution)/shard_map/all_gather | solution.py:27
  480.1 0.7 copy.21
  480.8 1.3 constant_dynamic-slice_fusion
  482.2 26.2 %copy.14 = bf16[16,4,512,256]{3,2,1,0:T(8,128)(2,1)} copy(bf16[16,4,512,256]{2,0,3,1:T(8,128)(2,1)} %bitcast.1) | data formatting | bytes 33554432 | tf_op jit(solution)/shard_map/all_to_all | solution.py:16
  508.3 0.0 all-to-all-done.1
  508.3 26.2 %copy.17 = bf16[16,4,512,256]{3,2,1,0:T(8,128)(2,1)} copy(bf16[16,4,512,256]{2,0,3,1:T(8,128)(2,1)} %bitcast.4) | data formatting | bytes 33554432 | tf_op jit(solution)/shard_map/all_to_all | solution.py:17
  (1 shorter events, 0.0 us)
Async XLA Ops:
  7.2 57.7 %all-reduce.3.cloned.1.call-start = ((), (), s32[]{:S(2)}) async-start(), calls=%async_computation.2 | async-start | bytes 262144 | tf_op jit(solution)/shard_map/pmax | solution.py:8
  7.2 20.2 %copy-start = (f32[16,512,1024]{2,1,0:T(8,128)S(1)}, f32[16,512,1024]{2,1,0:T(8,128)}, u32[]{:S(2)}) copy-start(f32[16,512,1024]{2,1,0:T(8,128)} %param.4) | copy-start | bytes 100663296
  83.6 190.3 %all-to-all-start = ((bf16[16,512,1024]{1,0,2:T(8,128)(2,1)}), bf16[16,512,1024]{1,0,2:T(8,128)(2,1)}, u32[]{:S(2)}, u32[]{:S(2)}) async-start(bf16[16,512,1024]{1,0,2:T(8,128)(2,1)} %divide_convert_fusion.1), calls=%async_computation | async-start | bytes 33554432 | tf_op jit(solution)/shard_map/all_to_all | solution.py:16
  90.7 34.2 %copy-start.1 = (f32[16,1024]{1,0:T(8,128)S(1)}, f32[16,1024]{1,0:T(8,128)}, u32[]{:S(2)}) copy-start(f32[16,1024]{1,0:T(8,128)} %get-tuple-element.6) | copy-start | bytes 196612
  125.1 155.7 %copy-start.2 = (f32[512,16]{0,1:T(8,128)S(1)}, f32[512,16]{0,1:T(8,128)}, u32[]{:S(2)}) copy-start(f32[512,16]{0,1:T(8,128)} %param.6) | copy-start | bytes 98308
  125.1 155.7 %copy-start.3 = (f32[512]{0:T(512)S(1)}, f32[512]{0:T(512)}, u32[]{:S(2)}) copy-start(f32[512]{0:T(512)} %param.7) | copy-start | bytes 6148
  273.9 234.4 %all-to-all-start.1 = ((bf16[16,512,1024]{1,0,2:T(8,128)(2,1)}), bf16[16,512,1024]{1,0,2:T(8,128)(2,1)}, u32[]{:S(2)}, u32[]{:S(2)}) async-start(bf16[16,512,1024]{1,0,2:T(8,128)(2,1)} %divide_convert_fusion), calls=%async_computation.1 | async-start | bytes 33554432 | tf_op jit(solution)/shard_map/all_to_all | solution.py:17
Sparse Core Ops, SparseCore 0:
  30.3 34.5 all-reduce.2
